TPU v7x, 512 devices: a whole 4x4x16 slice. The times are simulated.
512 devices in a mesh: grp: 4 (over x), dom: 128 (over z, y, core).
Axes of the slice: x: 4, y: 4, z: 16, core: 2. Of those that a mesh axis runs over, the one named last changes fastest.
Arguments:
- node_state: float32 [65536, 6, 128], P(('grp', 'dom')), may hold values from -6 to 6
- node_dest: int32 [65536], P(('grp', 'dom')), may hold values from 0 to 127, as said below
- seg_nodes: float32 [6, 262144], P(None, ('grp', 'dom')), may hold values from -6 to 6
- seg_conn: int32 [3, 524288], P(None, ('grp', 'dom')), may hold values from 0 to 511
- pair_seg: int32 [512, 4, 32], P(('grp', 'dom')), may hold values from 0 to 7
- pair_slot: int32 [512, 4, 32], P(('grp', 'dom')), may hold values from 0 to 255, as said below
Outputs:
- node_force: float32 [65536, 3, 128], P(('grp', 'dom'))
Inputs may be any that keep to these rules, and one draw needn't show every extreme that they name: `node_dest`: at most 2 blocks of one device name the same contact domain; in every grp row one contact domain receives exactly 2 blocks from every device of that row; every device sends at least one block to the contact domain of its own dom index. `pair_slot`: every entry names a slot d * 2 + k that holds a block: device (r, d) sends more than k blocks to the contact domain.
All inputs are finite; a program needn't handle non-finite values.
Results may differ from a plain program's by a relative error of at most 0.00023.
Values sent between devices are 32-bit elements; how exact they have to be, the bound alone decides.
No kernel may reach another device: no remote copies, remote signals or barrier semaphores. Data moves between devices by JAX's collectives and lax.ppermute only.
A program may use at most 64 MiB of HBM per device.

v0:
```python
import jax
import jax.numpy as jnp
from jax import lax
from jax.sharding import Mesh
from jax.sharding import PartitionSpec as P

SEG_BLK = 128
DOM = ("dom_0", "dom_1", "dom_2")
GRP_DOM = ("grp", "dom_0", "dom_1", "dom_2")
time_step = 0.5
stiffness = 0.5
radius_sq = 0.5


def in_blocks(shard, dim, devices):
    dims = shard.shape
    blocks = shard.reshape(*dims[:dim], devices, dims[dim] // devices, *dims[dim + 1 :])
    return jnp.moveaxis(blocks, dim, 0)


def in_order(blocks, dim):
    blocks = jnp.moveaxis(blocks, 0, dim)
    dims = blocks.shape
    return blocks.reshape(*dims[:dim], dims[dim] * dims[dim + 1], *dims[dim + 2 :])


def moved_by_axis(blocks, axes, turns):
    dims = [lax.axis_size(a) for a in axes]
    blocks = blocks.reshape(*dims, *blocks.shape[1:])
    for k in turns:
        blocks = lax.all_to_all(blocks, axes[k], split_axis=k, concat_axis=k, tiled=True)
    return blocks.reshape(-1, *blocks.shape[len(axes) :])


def two_step_exchange(shard, groups, turns, split_dim, concat_dim):
    devices = lax.axis_size(groups[0]) * lax.axis_size(groups[1])
    blocks = in_blocks(shard, split_dim, devices)
    return in_order(moved_by_axis(blocks, groups, turns), concat_dim)


def seg_geometry(corners):
    corner_a = corners[:, 0]
    corner_b = corners[:, 1]
    corner_c = corners[:, 2]
    edge_one = corner_b[0:3] - corner_a[0:3]
    edge_two = corner_c[0:3] - corner_a[0:3]
    normal = 0.5 * jnp.stack(
        [
            edge_one[1] * edge_two[2] - edge_one[2] * edge_two[1],
            edge_one[2] * edge_two[0] - edge_one[0] * edge_two[2],
            edge_one[0] * edge_two[1] - edge_one[1] * edge_two[0],
        ]
    )
    centre = (corner_a[0:3] + corner_b[0:3] + corner_c[0:3]) / 3.0
    motion = (corner_a[3:6] + corner_b[3:6] + corner_c[3:6]) / 3.0
    return jnp.concatenate([normal, centre, motion], axis=0)


def tile_force(node_rows, geometry):
    clearance = jnp.zeros((geometry.shape[1], node_rows.shape[1]), jnp.float32)
    distance = jnp.zeros((geometry.shape[1], node_rows.shape[1]), jnp.float32)
    for axis_id in range(3):
        offset = node_rows[axis_id][None, :] - geometry[3 + axis_id][:, None]
        drift = node_rows[3 + axis_id][None, :] - geometry[6 + axis_id][:, None]
        clearance = clearance + geometry[axis_id][:, None] * (offset + time_step * drift)
        distance = distance + offset * offset
    pressure = stiffness * jnp.exp(-distance / radius_sq) * jnp.maximum(-clearance, 0.0)
    return jnp.dot(
        geometry[0:3], pressure, precision=lax.Precision.HIGHEST, preferred_element_type=jnp.float32
    )


def place_rows(slot_ids, values, slot_total):
    onehot = (slot_ids[None, :] == jnp.arange(slot_total, dtype=jnp.int32)[:, None]).astype(
        jnp.float32
    )
    flattened = values.reshape(values.shape[0], -1)
    placed = jnp.dot(
        onehot, flattened, precision=lax.Precision.HIGHEST, preferred_element_type=jnp.float32
    )
    return placed.reshape((slot_total,) + values.shape[1:])


def shards(node_state, node_dest, seg_nodes, seg_conn, pair_seg, pair_slot):
    dom_count = lax.axis_size(DOM)
    grp_count = lax.axis_size("grp")
    block_count = node_state.shape[0]
    capacity = max(2, 2 * block_count // dom_count)
    slot_count = dom_count * capacity
    order_ids = jnp.arange(block_count, dtype=jnp.int32)
    earlier = order_ids[None, :] < order_ids[:, None]
    same_dom = node_dest[:, None] == node_dest[None, :]
    slot_rank = jnp.sum((same_dom & earlier).astype(jnp.int32), axis=1)
    target_slot = node_dest * capacity + slot_rank
    outgoing = place_rows(target_slot, node_state, slot_count)
    received = two_step_exchange(outgoing, (("dom_0", "dom_1"), "dom_2"), (1, 0), 0, 0)
    corners = jnp.take(seg_nodes, seg_conn, axis=1)
    geometry = seg_geometry(corners)
    seg_blocks = geometry.shape[1] // SEG_BLK
    geo_blocks = jnp.transpose(geometry.reshape(9, seg_blocks, SEG_BLK), (1, 0, 2))
    seg_table = pair_seg[0]
    slot_table = pair_slot[0]
    geo_all = lax.all_gather(geo_blocks, "grp", axis=0, tiled=True)
    seg_in, slot_in = (
        lax.all_to_all(seg_table, "grp", split_axis=0, concat_axis=0, tiled=True),
        lax.all_to_all(slot_table, "grp", split_axis=0, concat_axis=0, tiled=True),
    )
    owner_base = (jnp.arange(grp_count, dtype=jnp.int32) * seg_blocks)[:, None]
    seg_ids = (seg_in + owner_base).reshape(-1)
    slot_ids = slot_in.reshape(-1)
    forces = jax.vmap(tile_force)(
        jnp.take(received, slot_ids, axis=0), jnp.take(geo_all, seg_ids, axis=0)
    )
    own_forces = place_rows(slot_ids, forces, slot_count)
    returned = lax.all_to_all(own_forces, DOM, split_axis=0, concat_axis=0, tiled=True)
    return jnp.take(returned, target_slot, axis=0)


def solution(mesh):
    split = Mesh(
        mesh.devices.reshape(mesh.shape["grp"], 16, 4, 2), ("grp", "dom_0", "dom_1", "dom_2")
    )
    placed = (
        P(GRP_DOM, None, None),
        P(GRP_DOM),
        P(None, GRP_DOM),
        P(None, GRP_DOM),
        P(GRP_DOM, None, None),
        P(GRP_DOM, None, None),
    )
    return jax.shard_map(
        shards, mesh=split, in_specs=placed, out_specs=P(GRP_DOM, None, None), check_vma=False
    )
```

profile of v0, /device:TPU:33, one launch (start us, length us, event | category | flops | bytes accessed | tf_op | source)
XLA Modules:
  0.0 168.8 jit_solution(1052670801400604042)
XLA Ops:
  0.0 0.9 convert_reduce_fusion
  0.9 0.7 compare_and_fusion.3
  1.6 1.2 copy.65
  3.3 4.7 %all_to_all.39 = f32[64,2,2,6,128]{4,0,3,2,1:T(8,128)S(1)} all-to-all(f32[64,2,2,6,128]{4,0,3,2,1:T(8,128)S(1)} %fusion.34), channel_id=1, replica_groups=mesh['grp'=4,'dom_0'=16,'dom_1'=4,'dom_2'=2] {'dom_2'}, dimensions={1} | all-to-all | bytes 1572864 | tf_op jit(solution)/shard_map/all_to_all | solution.py:31
  8.0 4.0 %all-to-all-start.1 = ((s32[4,1,32]{2,1,0:T(1,128)}), s32[4,1,32]{2,1,0:T(1,128)S(1)}, u32[]{:S(2)}, u32[]{:S(2)}) async-start(s32[4,1,32]{2,1,0:T(1,128)} %bitcast.4), calls=%async_computation.1 | async-start | bytes 4096 | tf_op jit(solution)/shard_map/all_to_all | solution.py:105
  12.0 4.0 %all-to-all-done.1 = s32[4,1,32]{2,1,0:T(1,128)S(1)} async-done(((s32[4,1,32]{2,1,0:T(1,128)}), s32[4,1,32]{2,1,0:T(1,128)S(1)}, u32[]{:S(2)}, u32[]{:S(2)}) %all-to-all-start.1) | async-done | bytes 544 | tf_op jit(solution)/shard_map/all_to_all | solution.py:105
  16.0 3.2 %all-to-all-start = ((s32[4,1,32]{2,1,0:T(1,128)}), s32[4,1,32]{2,1,0:T(1,128)S(1)}, u32[]{:S(2)}, u32[]{:S(2)}) async-start(s32[4,1,32]{2,1,0:T(1,128)} %bitcast.1), calls=%async_computation | async-start | bytes 4096 | tf_op jit(solution)/shard_map/all_to_all | solution.py:106
  19.3 1.5 copy.66
  20.8 2.5 %all-to-all-done = s32[4,1,32]{2,1,0:T(1,128)S(1)} async-done(((s32[4,1,32]{2,1,0:T(1,128)}), s32[4,1,32]{2,1,0:T(1,128)S(1)}, u32[]{:S(2)}, u32[]{:S(2)}) %all-to-all-start) | async-done | bytes 544 | tf_op jit(solution)/shard_map/all_to_all | solution.py:106
  23.3 17.8 %all-to-all-start.3 = ((f32[64,2,2,6,128]{4,2,3,1,0:T(2,128)}), f32[64,2,2,6,128]{4,2,3,1,0:T(2,128)S(1)}, u32[]{:S(2)}, u32[]{:S(2)}) async-start(f32[64,2,2,6,128]{4,2,3,1,0:T(2,128)} %copy.66), calls=%async_computation.3 | async-start | bytes 1572864 | tf_op jit(solution)/shard_map/all_to_all | solution.py:31
  41.5 8.1 %gather_fusion = f32[3072,6]{1,0:T(8,128)S(1)} fusion(f32[6,512]{0,1:T(8,128)S(1)} %copy.62, s32[3072]{0:T(1024)S(1)} %broadcast_clamp_fusion), kind=kCustom, calls=%fused_computation | custom fusion | bytes 159744 | tf_op jit(solution)/shard_map/jit(_take)/gather | solution.py:97
  50.3 9.9 %all_gather.3 = f32[32,9,128]{2,0,1:T(8,128)S(1)} all-gather(f32[8,9,128]{2,0,1:T(8,128)S(1)} %maximum_bitcast_fusion), channel_id=1, replica_groups=mesh['grp'=4,'dom_0'=16,'dom_1'=4,'dom_2'=2] {'grp'}, dimensions={0}, use_global_device_ids=true | all-gather | bytes 184320 | tf_op jit(solution)/shard_map/all_gather | solution.py:103
  60.3 0.5 broadcast.150
  60.8 0.7 reduce.10
  61.7 0.7 reduce.11
  62.4 0.8 gather_fusion.1
  63.9 16.5 %all-to-all-done.3 = f32[64,2,2,6,128]{4,2,3,1,0:T(2,128)S(1)} async-done(((f32[64,2,2,6,128]{4,2,3,1,0:T(2,128)}), f32[64,2,2,6,128]{4,2,3,1,0:T(2,128)S(1)}, u32[]{:S(2)}, u32[]{:S(2)}) %all-to-all-start.3) | async-done | bytes 786464 | tf_op jit(solution)/shard_map/all_to_all | solution.py:31
  81.1 0.8 gather_fusion.2
  82.4 37.2 %fusion.14 = f32[128,3,128]{2,1,0:T(4,128)S(1)} fusion(f32[128,128]{1,0:T(8,128)S(1)} %bitcast.77, f32[128,128]{1,0:T(8,128)S(1)} %bitcast.86, f32[128,128]{1,0:T(8,128)S(1)} %bitcast.78, f32[128,128]{1,0:T(8,128)S(1)} %bitcast.79, f32[128,128]{1,0:T(8,128)S(1)} %bitcast.87, f32[128,128]{1,0:T(8,128)S(1)} %bitcast.80, f32[128,128]{1,0:T(8,128)S(1)} %bitcast.81, ...), kind=kOutput, calls=%fused_computation.24 | convolution fusion | flops 134217728 | bytes 1441792 | tf_op jit(solution)/shard_map/vmap()/dot_general | solution.py:68
  120.1 1.1 copy.70
  121.2 12.2 %all-to-all-start.4 = ((f32[256,3,128]{2,1,0:T(4,128)}), f32[256,3,128]{2,1,0:T(4,128)S(1)}, u32[]{:S(2)}, u32[]{:S(2)}) async-start(f32[256,3,128]{2,1,0:T(4,128)} %copy.70), calls=%async_computation.4 | async-start | bytes 1048576 | tf_op jit(solution)/shard_map/all_to_all | solution.py:115
  133.5 33.7 %all-to-all-done.4 = f32[256,3,128]{2,1,0:T(4,128)S(1)} async-done(((f32[256,3,128]{2,1,0:T(4,128)}), f32[256,3,128]{2,1,0:T(4,128)S(1)}, u32[]{:S(2)}, u32[]{:S(2)}) %all-to-all-start.4) | async-done | bytes 393248 | tf_op jit(solution)/shard_map/all_to_all | solution.py:115
  167.1 0.8 gather_fusion.3
  168.1 0.7 copy.71
  (44 shorter events, 4.5 us)
Async XLA Ops:
  2.7 9.2 %copy-start = (s32[3,1024]{1,0:T(4,128)S(1)}, s32[3,1024]{1,0:T(4,128)}, u32[]{:S(2)}) copy-start(s32[3,1024]{1,0:T(4,128)} %param.9) | copy-start | bytes 36868
  8.0 8.1 %all-to-all-start.1 = ((s32[4,1,32]{2,1,0:T(1,128)}), s32[4,1,32]{2,1,0:T(1,128)S(1)}, u32[]{:S(2)}, u32[]{:S(2)}) async-start(s32[4,1,32]{2,1,0:T(1,128)} %bitcast.4), calls=%async_computation.1 | async-start | bytes 4096 | tf_op jit(solution)/shard_map/all_to_all | solution.py:105
  16.0 7.3 %all-to-all-start = ((s32[4,1,32]{2,1,0:T(1,128)}), s32[4,1,32]{2,1,0:T(1,128)S(1)}, u32[]{:S(2)}, u32[]{:S(2)}) async-start(s32[4,1,32]{2,1,0:T(1,128)} %bitcast.1), calls=%async_computation | async-start | bytes 4096 | tf_op jit(solution)/shard_map/all_to_all | solution.py:106
  19.3 22.1 %copy-start.1 = (f32[6,512]{1,0:T(8,128)S(1)}, f32[6,512]{1,0:T(8,128)}, u32[]{:S(2)}) copy-start(f32[6,512]{1,0:T(8,128)} %param.8) | copy-start | bytes 36868
  23.3 57.1 %all-to-all-start.3 = ((f32[64,2,2,6,128]{4,2,3,1,0:T(2,128)}), f32[64,2,2,6,128]{4,2,3,1,0:T(2,128)S(1)}, u32[]{:S(2)}, u32[]{:S(2)}) async-start(f32[64,2,2,6,128]{4,2,3,1,0:T(2,128)} %copy.66), calls=%async_computation.3 | async-start | bytes 1572864 | tf_op jit(solution)/shard_map/all_to_all | solution.py:31
  121.2 46.0 %all-to-all-start.4 = ((f32[256,3,128]{2,1,0:T(4,128)}), f32[256,3,128]{2,1,0:T(4,128)S(1)}, u32[]{:S(2)}, u32[]{:S(2)}) async-start(f32[256,3,128]{2,1,0:T(4,128)} %copy.70), calls=%async_computation.4 | async-start | bytes 1048576 | tf_op jit(solution)/shard_map/all_to_all | solution.py:115
where the time goes:
time: 169 us
  waiting for transfers between devices  56.7 us (34%)
  matrix products  38.1 us (23%)
  starting transfers between devices  37.3 us (22%)
  local copies, waits for them, and re-layouts  18.2 us (11%)
  blocking collectives  14.5 us (9%)
  other arithmetic  3.67 us (2%)
    dot_general x1, matrix products, tile_force(): jnp.dot(geometry[0:3], pressure, precision=lax.Precision.HIGHEST, preferr...  37.2 us
    all_to_all x1, waiting for transfers between devices, shards(): lax.all_to_all(own_forces, DOM, split_axis=0, concat_axis=0, tiled=True)  33.7 us
    all_to_all x1, starting transfers between devices, moved_by_axis(): lax.all_to_all(blocks, axes[k], split_axis=k, concat_axis=k, tiled=True)  17.8 us
    all_to_all x1, waiting for transfers between devices, moved_by_axis(): lax.all_to_all(blocks, axes[k], split_axis=k, concat_axis=k, tiled=True)  16.5 us
    all_to_all x1, starting transfers between devices, shards(): lax.all_to_all(own_forces, DOM, split_axis=0, concat_axis=0, tiled=True)  12.2 us
    all_gather x1, blocking collectives, shards(): geo_all = lax.all_gather(geo_blocks, 'grp', axis=0, tiled=True)  9.87 us
    gather x2, local copies, waits for them, and re-layouts, shards(): corners = jnp.take(seg_nodes, seg_conn, axis=1)  8.59 us
    all_to_all x1, blocking collectives, moved_by_axis(): lax.all_to_all(blocks, axes[k], split_axis=k, concat_axis=k, tiled=True)  4.67 us
  transfers between devices with their start and end apart: 4, of which 4 were waited for; matrix products, arithmetic and copies ran while one was open for 8% of the time, Pallas kernels for 0%

commit v1 on v0

--- a/solution.py
+++ b/solution.py
@@ -10,6 +10,22 @@
 time_step = 0.5
 stiffness = 0.5
 radius_sq = 0.5
+
+
+def pairwise_exchange(x, axis, split, join):
+    ways, here = (lax.axis_size(axis), lax.axis_index(axis))
+    width = x.shape[split] // ways
+    shape = list(x.shape)
+    shape[split] = width
+    height = shape[join]
+    shape[join] = height * ways
+    full = jnp.zeros(shape, x.dtype)
+    for mask in range(ways):
+        part = lax.dynamic_slice_in_dim(x, (here ^ mask) * width, width, axis=split)
+        if mask:
+            part = lax.ppermute(part, axis, [(d, d ^ mask) for d in range(ways)])
+        full = lax.dynamic_update_slice_in_dim(full, part, (here ^ mask) * height, axis=join)
+    return full
 
 
 def in_blocks(shard, dim, devices):
@@ -102,7 +118,7 @@
     slot_table = pair_slot[0]
     geo_all = lax.all_gather(geo_blocks, "grp", axis=0, tiled=True)
     seg_in, slot_in = (
-        lax.all_to_all(seg_table, "grp", split_axis=0, concat_axis=0, tiled=True),
+        pairwise_exchange(seg_table, "grp", 0, 0),
         lax.all_to_all(slot_table, "grp", split_axis=0, concat_axis=0, tiled=True),
     )
     owner_base = (jnp.arange(grp_count, dtype=jnp.int32) * seg_blocks)[:, None]

time: 169 us -> 183 us (1.083)
  the two profiles are of different devices: /device:TPU:33 before, /device:TPU:39 now
where the time goes in v1:
time: 183 us; the launch traced here: 182 us
  waiting for transfers between devices  62.9 us (34%)
  starting transfers between devices  41.1 us (22%)
  matrix products  38 us (21%)
  local copies, waits for them, and re-layouts  20.7 us (11%)
  blocking collectives  16.1 us (9%)
  other arithmetic  3.13 us (2%)
    dot_general x1, matrix products, tile_force(): jnp.dot(geometry[0:3], pressure, precision=lax.Precision.HIGHEST, preferr...  37.1 us
    all_to_all x1, waiting for transfers between devices, shards(): lax.all_to_all(own_forces, DOM, split_axis=0, concat_axis=0, tiled=True)  33.7 us
    all_to_all x1, waiting for transfers between devices, moved_by_axis(): lax.all_to_all(blocks, axes[k], split_axis=k, concat_axis=k, tiled=True)  29.2 us
    all_to_all x1, starting transfers between devices, moved_by_axis(): lax.all_to_all(blocks, axes[k], split_axis=k, concat_axis=k, tiled=True)  17.8 us
    all_gather x1, blocking collectives, shards(): geo_all = lax.all_gather(geo_blocks, 'grp', axis=0, tiled=True)  10 us
    ppermute x3, starting transfers between devices, pairwise_exchange(): part = lax.ppermute(part, axis, [(d, d ^ mask) for d in range(ways)])  9.57 us
    all_to_all x1, starting transfers between devices, shards(): lax.all_to_all(own_forces, DOM, split_axis=0, concat_axis=0, tiled=True)  9.48 us
    gather x2, local copies, waits for them, and re-layouts, shards(): corners = jnp.take(seg_nodes, seg_conn, axis=1)  8.59 us
  transfers between devices with their start and end apart: 6, of which 2 were waited for; matrix products, arithmetic and copies ran while one was open for 10% of the time, Pallas kernels for 0%

profile of v1, /device:TPU:39, one launch (start us, length us, event | category | flops | bytes accessed | tf_op | source)
XLA Modules:
  0.0 182.2 jit_solution(963501544666832464)
XLA Ops:
  0.0 4.2 %all-to-all-start = ((s32[4,1,32]{2,1,0:T(1,128)}), s32[4,1,32]{2,1,0:T(1,128)S(1)}, u32[]{:S(2)}, u32[]{:S(2)}) async-start(s32[4,1,32]{2,1,0:T(1,128)} %bitcast.99), calls=%async_computation | async-start | bytes 4096 | tf_op jit(solution)/shard_map/all_to_all | solution.py:122
  4.2 0.8 fusion.52
  5.0 1.9 %collective-permute-start.2 = (s32[1,32]{1,0:T(1,128)S(1)}, s32[1,32]{1,0:T(1,128)S(1)}, u32[]{:S(2)}, u32[]{:S(2)}) collective-permute-start(s32[1,32]{1,0:T(1,128)S(1)} %get-tuple-element.29), channel_id=1, source_target_pairs={{0,384},{128,256},{256,128},{384,0},{1,385},{129,257},{257,129},{3... | collective-permute-start | bytes 392 | tf_op jit(solution)/shard_map/ppermute | solution.py:26
  7.0 2.8 %collective-permute-start = (s32[1,32]{1,0:T(1,128)S(1)}, s32[1,32]{1,0:T(1,128)S(1)}, u32[]{:S(2)}, u32[]{:S(2)}) collective-permute-start(s32[1,32]{1,0:T(1,128)S(1)} %get-tuple-element.30), channel_id=1, source_target_pairs={{0,128},{128,0},{256,384},{384,256},{1,129},{129,1},{257,385},{385... | collective-permute-start | bytes 392 | tf_op jit(solution)/shard_map/ppermute | solution.py:26
  9.7 4.9 %collective-permute-start.1 = (s32[1,32]{1,0:T(1,128)S(1)}, s32[1,32]{1,0:T(1,128)S(1)}, u32[]{:S(2)}, u32[]{:S(2)}) collective-permute-start(s32[1,32]{1,0:T(1,128)S(1)} %get-tuple-element.32), channel_id=1, source_target_pairs={{0,256},{128,384},{256,0},{384,128},{1,257},{129,385},{257,1},{385... | collective-permute-start | bytes 392 | tf_op jit(solution)/shard_map/ppermute | solution.py:26
  14.7 0.9 convert_reduce_fusion
  15.6 0.7 compare_select_fusion
  16.3 0.9 copy.59
  17.2 1.2 copy.62
  18.4 8.1 %gather_fusion = f32[3072,6]{1,0:T(8,128)S(1)} fusion(f32[6,512]{0,1:T(8,128)S(1)} %copy.59, s32[3072]{0:T(1024)S(1)} %broadcast_clamp_fusion), kind=kCustom, calls=%fused_computation | custom fusion | bytes 159744 | tf_op jit(solution)/shard_map/jit(_take)/gather | solution.py:113
  28.8 6.1 %all_to_all.24 = f32[64,2,2,6,128]{4,0,3,2,1:T(8,128)S(1)} all-to-all(f32[64,2,2,6,128]{4,0,3,2,1:T(8,128)S(1)} %fusion.34), channel_id=1, replica_groups=mesh['grp'=4,'dom_0'=16,'dom_1'=4,'dom_2'=2] {'dom_2'}, dimensions={1} | all-to-all | bytes 1572864 | tf_op jit(solution)/shard_map/all_to_all | solution.py:47
  34.8 1.5 copy.63
  36.4 17.8 %all-to-all-start.2 = ((f32[64,2,2,6,128]{4,2,3,1,0:T(2,128)}), f32[64,2,2,6,128]{4,2,3,1,0:T(2,128)S(1)}, u32[]{:S(2)}, u32[]{:S(2)}) async-start(f32[64,2,2,6,128]{4,2,3,1,0:T(2,128)} %copy.63), calls=%async_computation.2 | async-start | bytes 1572864 | tf_op jit(solution)/shard_map/all_to_all | solution.py:47
  54.4 10.0 %all_gather.3 = f32[32,9,128]{2,0,1:T(8,128)S(1)} all-gather(f32[8,9,128]{2,0,1:T(8,128)S(1)} %maximum_bitcast_fusion), channel_id=1, replica_groups=mesh['grp'=4,'dom_0'=16,'dom_1'=4,'dom_2'=2] {'grp'}, dimensions={0}, use_global_device_ids=true | all-gather | bytes 184320 | tf_op jit(solution)/shard_map/all_gather | solution.py:119
  64.9 0.8 gather_fusion.1
  65.9 1.0 fusion.58
  67.0 29.2 %all-to-all-done.2 = f32[64,2,2,6,128]{4,2,3,1,0:T(2,128)S(1)} async-done(((f32[64,2,2,6,128]{4,2,3,1,0:T(2,128)}), f32[64,2,2,6,128]{4,2,3,1,0:T(2,128)S(1)}, u32[]{:S(2)}, u32[]{:S(2)}) %all-to-all-start.2) | async-done | bytes 786464 | tf_op jit(solution)/shard_map/all_to_all | solution.py:47
  97.0 0.8 gather_fusion.2
  98.7 37.1 %fusion.14 = f32[128,3,128]{2,1,0:T(4,128)S(1)} fusion(f32[128,128]{1,0:T(8,128)S(1)} %bitcast.81, f32[128,128]{1,0:T(8,128)S(1)} %bitcast.90, f32[128,128]{1,0:T(8,128)S(1)} %bitcast.82, f32[128,128]{1,0:T(8,128)S(1)} %bitcast.83, f32[128,128]{1,0:T(8,128)S(1)} %bitcast.91, f32[128,128]{1,0:T(8,128)S(1)} %bitcast.84, f32[128,128]{1,0:T(8,128)S(1)} %bitcast.85, ...), kind=kOutput, calls=%fused_computation.24 | convolution fusion | flops 134217728 | bytes 1441792 | tf_op jit(solution)/shard_map/vmap()/dot_general | solution.py:84
  136.3 1.1 copy.67
  137.4 9.5 %all-to-all-start.3 = ((f32[256,3,128]{2,1,0:T(4,128)}), f32[256,3,128]{2,1,0:T(4,128)S(1)}, u32[]{:S(2)}, u32[]{:S(2)}) async-start(f32[256,3,128]{2,1,0:T(4,128)} %copy.67), calls=%async_computation.3 | async-start | bytes 1048576 | tf_op jit(solution)/shard_map/all_to_all | solution.py:131
  146.9 33.7 %all-to-all-done.3 = f32[256,3,128]{2,1,0:T(4,128)S(1)} async-done(((f32[256,3,128]{2,1,0:T(4,128)}), f32[256,3,128]{2,1,0:T(4,128)S(1)}, u32[]{:S(2)}, u32[]{:S(2)}) %all-to-all-start.3) | async-done | bytes 393248 | tf_op jit(solution)/shard_map/all_to_all | solution.py:131
  180.6 0.8 gather_fusion.3
  181.5 0.7 copy.68
  (56 shorter events, 5.5 us)
Async XLA Ops:
  0.0 27.0 %all-to-all-start = ((s32[4,1,32]{2,1,0:T(1,128)}), s32[4,1,32]{2,1,0:T(1,128)S(1)}, u32[]{:S(2)}, u32[]{:S(2)}) async-start(s32[4,1,32]{2,1,0:T(1,128)} %bitcast.99), calls=%async_computation | async-start | bytes 4096 | tf_op jit(solution)/shard_map/all_to_all | solution.py:122
  5.0 59.6 %collective-permute-start.2 = (s32[1,32]{1,0:T(1,128)S(1)}, s32[1,32]{1,0:T(1,128)S(1)}, u32[]{:S(2)}, u32[]{:S(2)}) collective-permute-start(s32[1,32]{1,0:T(1,128)S(1)} %get-tuple-element.29), channel_id=1, source_target_pairs={{0,384},{128,256},{256,128},{384,0},{1,385},{129,257},{257,129},{3... | collective-permute-start | bytes 392 | tf_op jit(solution)/shard_map/ppermute | solution.py:26
  7.0 57.6 %collective-permute-start = (s32[1,32]{1,0:T(1,128)S(1)}, s32[1,32]{1,0:T(1,128)S(1)}, u32[]{:S(2)}, u32[]{:S(2)}) collective-permute-start(s32[1,32]{1,0:T(1,128)S(1)} %get-tuple-element.30), channel_id=1, source_target_pairs={{0,128},{128,0},{256,384},{384,256},{1,129},{129,1},{257,385},{385... | collective-permute-start | bytes 392 | tf_op jit(solution)/shard_map/ppermute | solution.py:26
  9.7 54.9 %collective-permute-start.1 = (s32[1,32]{1,0:T(1,128)S(1)}, s32[1,32]{1,0:T(1,128)S(1)}, u32[]{:S(2)}, u32[]{:S(2)}) collective-permute-start(s32[1,32]{1,0:T(1,128)S(1)} %get-tuple-element.32), channel_id=1, source_target_pairs={{0,256},{128,384},{256,0},{384,128},{1,257},{129,385},{257,1},{385... | collective-permute-start | bytes 392 | tf_op jit(solution)/shard_map/ppermute | solution.py:26
  17.2 11.1 %copy-start.4 = (s32[128]{0:T(128)S(1)}, s32[128]{0:T(128)}, u32[]{:S(2)}) copy-start(s32[128]{0:T(128)} %param.7) | copy-start | bytes 1540
  34.8 19.4 %copy-start.3 = (s32[3,1024]{1,0:T(4,128)S(1)}, s32[3,1024]{1,0:T(4,128)}, u32[]{:S(2)}) copy-start(s32[3,1024]{1,0:T(4,128)} %param.9) | copy-start | bytes 36868
  36.4 59.9 %all-to-all-start.2 = ((f32[64,2,2,6,128]{4,2,3,1,0:T(2,128)}), f32[64,2,2,6,128]{4,2,3,1,0:T(2,128)S(1)}, u32[]{:S(2)}, u32[]{:S(2)}) async-start(f32[64,2,2,6,128]{4,2,3,1,0:T(2,128)} %copy.63), calls=%async_computation.2 | async-start | bytes 1572864 | tf_op jit(solution)/shard_map/all_to_all | solution.py:47
  97.8 0.8 copy-start
  97.8 0.9 copy-start.1
  97.8 0.9 copy-start.2
  137.4 43.2 %all-to-all-start.3 = ((f32[256,3,128]{2,1,0:T(4,128)}), f32[256,3,128]{2,1,0:T(4,128)S(1)}, u32[]{:S(2)}, u32[]{:S(2)}) async-start(f32[256,3,128]{2,1,0:T(4,128)} %copy.67), calls=%async_computation.3 | async-start | bytes 1048576 | tf_op jit(solution)/shard_map/all_to_all | solution.py:131
